TPU v7x, 32 devices: a whole 2x2x4 slice. The times are simulated.
32 devices in a mesh: dp: 2 (over y), row: 4 (over x, core), col: 4 (over z).
Axes of the slice: x: 2, y: 2, z: 4, core: 2. Of those that a mesh axis runs over, the one named last changes fastest.
Arguments:
- tokens: bfloat16 [2048, 8192], P(('dp', 'col'), 'row'), may hold values from -6 to 6
- frozen_weight: bfloat16 [8192, 8192], P('row', 'col'), may hold values from -0.0625 to 0.0625
- input_adapter_factor: bfloat16 [16, 8192], P(None, 'row'), may hold values from -0.0625 to 0.0625
- output_adapter_factor: bfloat16 [16, 8192], P(None, 'col'), may hold values from -1.5 to 1.5
- magnitude: float32 [8192], P('col'), may hold values from 0.5 to 2
- cotangent: bfloat16 [2048, 8192], P(('dp', 'row'), 'col'), may hold values from -6 to 6
- sequence_lengths: int32 [2, 8], P('dp'), may hold values from 1 to 512, 1024 in all within a row
Outputs:
- projected: bfloat16 [2048, 8192], P(('dp', 'row'), 'col')
- grad_mag: float32 [8192], P('col')
- input_factor_gradient: float32 [16, 8192], P(None, 'row')
- grad_b: float32 [16, 8192], P(None, 'col')
Inputs may be any that keep to these rules, and one draw needn't show every extreme that they name: `sequence_lengths`: each group's 8 lengths sum to 1024, and one of them is exactly 512.
All inputs are finite; a program needn't handle non-finite values.
Results may differ from a plain program's by a relative error of at most 0.0052.
Values may be sent and summed in bfloat16 or wider, within the bound.
No kernel may reach another device: no remote copies, remote signals or barrier semaphores. Data moves between devices by JAX's collectives and lax.ppermute only.
A program may use at most 64 MiB of HBM per device.

v0:
```python
import jax
import jax.numpy as jnp
from jax import lax
from jax.sharding import PartitionSpec as P

norm_eps = 1e-06
highest_precision = lax.Precision.HIGHEST


def contract_product(left, right, left_dim, right_dim):
    return lax.dot_general(
        left, right, (((left_dim,), (right_dim,)), ((), ())), preferred_element_type=jnp.float32
    )


def per_device(
    tokens,
    frozen_weight,
    input_adapter_factor,
    output_adapter_factor,
    magnitude,
    cotangent,
    sequence_lengths,
):
    row_count = lax.axis_size("row")
    col_count = lax.axis_size("col")
    row_index = lax.axis_index("row")
    col_index = lax.axis_index("col")
    group_index = lax.axis_index("dp")
    local_rows = tokens.shape[0]
    group_rows = local_rows * col_count
    block_rows = group_rows // row_count
    adapter_rank_size = input_adapter_factor.shape[0]
    low_rank_update = contract_product(input_adapter_factor, output_adapter_factor, 0, 0)
    merged = frozen_weight.astype(jnp.float32) + low_rank_update
    norm_terms = jnp.sum(merged * merged, axis=0)
    gram_partial_terms = contract_product(input_adapter_factor, input_adapter_factor, 1, 1)
    merged_factor_terms = jnp.dot(
        input_adapter_factor, frozen_weight, preferred_element_type=jnp.float32
    ) + jnp.dot(
        gram_partial_terms, output_adapter_factor.astype(jnp.float32), precision=highest_precision
    )
    portion = lax.all_gather(tokens, "col", axis=0, tiled=True)
    base_piece = jnp.dot(portion, frozen_weight, preferred_element_type=jnp.float32)
    down_portion = contract_product(portion, input_adapter_factor, 1, 1)
    frozen_rows, down_rows = (
        lax.psum_scatter(base_piece, "row", scatter_dimension=0, tiled=True),
        lax.psum_scatter(down_portion, "row", scatter_dimension=0, tiled=True),
    )
    norm_sq, merged_input_factor = lax.psum((norm_terms, merged_factor_terms), "row")
    down_activations = down_rows.astype(jnp.bfloat16)
    col_norm = jnp.sqrt(norm_sq + norm_eps)
    col_scale = magnitude / col_norm
    query_projection = frozen_rows + jnp.dot(
        down_activations, output_adapter_factor, preferred_element_type=jnp.float32
    )
    projected = (query_projection * col_scale[None, :]).astype(jnp.bfloat16)
    lengths = sequence_lengths[0]
    ends = jnp.cumsum(lengths, dtype=jnp.int32)
    starts = ends - lengths
    positions = row_index * block_rows + jnp.arange(block_rows, dtype=jnp.int32)
    inside = (positions[:, None] >= starts[None, :]) & (positions[:, None] < ends[None, :])
    inverse = 1.0 / lengths.astype(jnp.float32)
    weights = jnp.sum(jnp.where(inside, inverse[None, :], jnp.float32(0.0)), axis=1)
    grad_out = cotangent.astype(jnp.float32) * weights[:, None]
    scale_terms = jnp.sum(grad_out * query_projection, axis=0)
    projection_gradient = (grad_out * col_scale[None, :]).astype(jnp.bfloat16)
    bgrad_terms = contract_product(down_activations, projection_gradient, 0, 0)
    scale_grad, bgrad_data = lax.psum((scale_terms, bgrad_terms), ("dp", "row"))
    grad_mag = scale_grad / col_norm
    norm_coefficient = -scale_grad * magnitude / (col_norm * col_norm * col_norm)
    grad_b = bgrad_data + merged_input_factor * norm_coefficient[None, :]
    backward_terms = contract_product(projection_gradient, output_adapter_factor, 1, 1)
    padded = lax.dynamic_update_slice_in_dim(
        jnp.zeros((group_rows, adapter_rank_size), jnp.float32),
        backward_terms,
        row_index * block_rows,
        0,
    )
    backward_rows = lax.psum(padded, ("row", "col")).astype(jnp.bfloat16)
    back_mine = lax.dynamic_slice_in_dim(backward_rows, col_index * local_rows, local_rows, 0)
    row_term = contract_product(back_mine, tokens, 0, 0)
    scaled_output_factor = (
        output_adapter_factor.astype(jnp.float32) * norm_coefficient[None, :]
    ).astype(jnp.bfloat16)
    norm_term = contract_product(scaled_output_factor, frozen_weight, 1, 1) + jnp.dot(
        contract_product(scaled_output_factor, output_adapter_factor, 1, 1),
        input_adapter_factor.astype(jnp.float32),
        precision=highest_precision,
    )
    first_group = (group_index == 0).astype(jnp.float32)
    input_factor_gradient = lax.psum(row_term + first_group * norm_term, ("dp", "col"))
    return (projected, grad_mag, input_factor_gradient, grad_b)


def solution(mesh):
    in_specs = (
        P(("dp", "col"), "row"),
        P("row", "col"),
        P(None, "row"),
        P(None, "col"),
        P("col"),
        P(("dp", "row"), "col"),
        P("dp", None),
    )
    out_specs = (P(("dp", "row"), "col"), P("col"), P(None, "row"), P(None, "col"))
    return jax.shard_map(
        per_device, mesh=mesh, in_specs=in_specs, out_specs=out_specs, check_vma=False
    )
```

profile of v0, /device:TPU:0, one launch (start us, length us, event | category | flops | bytes accessed | tf_op | source)
XLA Modules:
  0.0 366.2 jit_solution(13270679273868545477)
XLA Ops:
  7.2 0.0 all-gather.2.cloned.1.call-start
  7.2 0.7 all-gather.2.cloned.1.call-update
  7.9 0.0 reduce-scatter.5.cloned.1.call-start
  8.0 85.1 %all-gather.2.cloned.1.call-done = bf16[1024,2048]{1,0:T(8,128)(2,1)} async-done(((bf16[256,2048]{1,0:T(8,128)(2,1)}), bf16[1024,2048]{1,0:T(8,128)(2,1)}) %all-gather.2.cloned.1.call-update) | async-done | bytes 4194320 | tf_op jit(solution)/shard_map/all_gather | solution.py:43
  93.1 4.0 %fusion.14 = f32[1024,16]{0,1:T(8,128)} fusion(bf16[1024,2048]{1,0:T(8,128)(2,1)} %all-gather.2.cloned.1.call-done, bf16[16,2048]{1,0:T(8,128)(2,1)S(1)} %copy-done), kind=kOutput, calls=%fused_computation.33 | convolution fusion | flops 67108864 | bytes 4325376 | tf_op jit(solution)/shard_map/dot_general | solution.py:11
  97.1 0.0 reduce-scatter.3.cloned.1.call-start
  97.1 14.4 %fusion.13 = f32[1024,2048]{1,0:T(8,128)} fusion(bf16[1024,2048]{1,0:T(8,128)(2,1)} %all-gather.2.cloned.1.call-done, bf16[2048,2048]{1,0:T(8,128)(2,1)} %param.8), kind=kOutput, calls=%fused_computation.32 | convolution fusion | flops 8589934592 | bytes 20971520 | tf_op jit(solution)/shard_map/dot_general | solution.py:44
  111.6 0.0 all-reduce.8.cloned.1.call-start
  111.6 0.1 fusion.16
  111.8 4.6 %fusion.15 = f32[16,2048]{1,0:T(8,128)S(1)} fusion(bf16[16,2048]{1,0:T(8,128)(2,1)S(1)} %copy-done, bf16[2048,2048]{1,0:T(8,128)(2,1)} %param.8), kind=kOutput, calls=%fused_computation.34 | convolution fusion | flops 134217728 | bytes 8585216 | tf_op jit(solution)/shard_map/dot_general | solution.py:38
  116.4 0.9 convolution_add_fusion.1
  117.3 0.0 all-reduce.6.cloned.1.call-start
  117.4 5.9 %multiply_reduce_fusion = f32[2048]{0:T(1024)S(1)} fusion(bf16[2048,2048]{1,0:T(8,128)(2,1)} %param.8, bf16[16,2048]{1,0:T(8,128)(2,1)S(1)} %copy-done, bf16[16,2048]{1,0:T(8,128)(2,1)S(1)} %copy-done.2), kind=kOutput, calls=%fused_computation | convolution fusion | flops 150992896 | bytes 8527872 | tf_op jit(solution)/shard_map/dot_general | solution.py:11
  123.3 0.2 reduce-window.4
  123.5 6.5 %psum.42 = f32[2048]{0:T(1024)S(1)} all-reduce(f32[2048]{0:T(1024)S(1)} %multiply_reduce_fusion), channel_id=1, replica_groups=mesh['dp'=2,'row'=4,'col'=4] {'row'}, use_global_device_ids=true, to_apply=%region_3.0 | all-reduce | flops 2048 | bytes 16384 | tf_op jit(solution)/shard_map/psum | solution.py:50
  130.1 0.1 select_reduce_fusion
  130.2 0.5 convolution_dynamic-update-slice_fusion
  130.7 69.2 %psum.44 = bf16[1024,16]{1,0:T(8,128)(2,1)S(1)} all-reduce(f32[1024,16]{1,0:T(8,128)S(1)} %convolution_dynamic-update-slice_fusion), channel_id=1, replica_groups=mesh['dp'=2,'row'=4,'col'=4] {'row','col'}, use_global_device_ids=true, to_apply=%region_8.9 | all-reduce | flops 16384 | bytes 98304 | tf_op jit(solution)/shard_map/psum | solution.py:80
  200.0 1.8 fusion.1
  201.8 0.0 all-reduce.4.cloned.1.call-start
  201.9 3.2 multiply_reduce_fusion.1
  205.1 12.1 %psum.43 = f32[2048]{0:T(1024)S(1)} all-reduce(f32[2048]{0:T(1024)S(1)} %get-tuple-element.4), channel_id=1, replica_groups=mesh['dp'=2,'row'=4,'col'=4] {'dp','row'}, use_global_device_ids=true, to_apply=%region_7.8 | all-reduce | flops 2048 | bytes 16384 | tf_op jit(solution)/shard_map/psum | solution.py:69
  217.1 0.6 fusion.6
  217.8 5.7 %fusion.3 = f32[16,2048]{1,0:T(8,128)S(1)} fusion(bf16[2048,2048]{1,0:T(8,128)(2,1)} %param.8, bf16[16,2048]{1,0:T(8,128)(2,1)S(1)} %copy-done.2, f32[2048]{0:T(1024)S(1)} %get-tuple-element.6), kind=kOutput, calls=%fused_computation.16 | convolution fusion | flops 134316032 | bytes 8593408 | tf_op jit(solution)/shard_map/dot_general | solution.py:11
  223.5 0.1 fusion.2
  223.6 0.2 fusion
  223.9 0.9 convolution_add_fusion.3
  224.8 2.4 all-reduce.8.cloned.1.call-done
  227.2 57.0 %all-reduce.6.cloned.1.call-done = f32[16,2048]{1,0:T(8,128)} async-done(((f32[16,2048]{1,0:T(8,128)}), f32[16,2048]{1,0:T(8,128)}) %all-reduce.6.cloned.1.call-update) | async-done | bytes 131088 | tf_op jit(solution)/shard_map/psum | solution.py:69
  284.2 1.6 multiply_add_fusion
  285.9 71.9 %all-reduce.4.cloned.1.call-done = f32[16,2048]{1,0:T(8,128)} async-done(((f32[16,2048]{1,0:T(8,128)}), f32[16,2048]{1,0:T(8,128)}) %all-reduce.4.cloned.1.call-update) | async-done | bytes 131088 | tf_op jit(solution)/shard_map/psum | solution.py:92
  357.8 1.6 copy.15
  (24 shorter events, 0.2 us)
Async XLA Ops:
  7.2 85.9 %copy-start = (bf16[16,2048]{1,0:T(8,128)(2,1)S(1)}, bf16[16,2048]{1,0:T(8,128)(2,1)}, u32[]{:S(2)}) copy-start(bf16[16,2048]{1,0:T(8,128)(2,1)} %param.9) | copy-start | bytes 196612
  7.2 85.9 %all-gather.2.cloned.1.call-start = ((), (), s32[]{:S(2)}) async-start(), calls=%async_computation.2 | async-start | bytes 5242880 | tf_op jit(solution)/shard_map/all_gather | solution.py:43
  7.9 192.0 %reduce-scatter.5.cloned.1.call-start = ((), (), s32[]{:S(2)}) async-start(), calls=%async_computation.4 | async-start | bytes 81920 | tf_op jit(solution)/shard_map/reduce_scatter | solution.py:48
  97.1 104.8 %reduce-scatter.3.cloned.1.call-start = ((), (), s32[]{:S(2)}) async-start(), calls=%async_computation.3 | async-start | bytes 10485760 | tf_op jit(solution)/shard_map/reduce_scatter | solution.py:47
  111.6 115.7 %all-reduce.8.cloned.1.call-start = ((), (), s32[]{:S(2)}) async-start(), calls=%async_computation.7 | async-start | bytes 262144 | tf_op jit(solution)/shard_map/psum | solution.py:50
  111.8 4.6 %copy-start.2 = (bf16[16,2048]{1,0:T(8,128)(2,1)S(1)}, bf16[16,2048]{1,0:T(8,128)(2,1)}, u32[]{:S(2)}) copy-start(bf16[16,2048]{1,0:T(8,128)(2,1)} %param.10) | copy-start | bytes 196612
  117.3 166.9 %all-reduce.6.cloned.1.call-start = ((), (), s32[]{:S(2)}) async-start(), calls=%async_computation.6 | async-start | bytes 262144 | tf_op jit(solution)/shard_map/psum | solution.py:69
  117.3 5.9 %copy-start.5 = (s32[1,8]{1,0:T(1,128)S(1)}, s32[1,8]{1,0:T(1,128)}, u32[]{:S(2)}) copy-start(s32[1,8]{1,0:T(1,128)} %param.13) | copy-start | bytes 100
  117.4 12.7 %copy-start.4 = (f32[2048]{0:T(1024)S(1)}, f32[2048]{0:T(1024)}, u32[]{:S(2)}) copy-start(f32[2048]{0:T(1024)} %param.11) | copy-start | bytes 24580
  117.4 12.8 %copy-start.3 = (bf16[256,2048]{1,0:T(8,128)(2,1)S(1)}, bf16[256,2048]{1,0:T(8,128)(2,1)}, u32[]{:S(2)}) copy-start(bf16[256,2048]{1,0:T(8,128)(2,1)} %param.12) | copy-start | bytes 3145732
  201.8 156.0 %all-reduce.4.cloned.1.call-start = ((), (), s32[]{:S(2)}) async-start(), calls=%async_computation.5 | async-start | bytes 262144 | tf_op jit(solution)/shard_map/psum | solution.py:92
  217.8 6.1 %copy-start.1 = (bf16[256,2048]{1,0:T(8,128)(2,1)S(1)}, bf16[256,2048]{1,0:T(8,128)(2,1)}, u32[]{:S(2)}) copy-start(bf16[256,2048]{1,0:T(8,128)(2,1)} %param.7) | copy-start | bytes 3145732
Sparse Core Ops, SparseCore 0:
  9.6 83.4 all-gather.1
  97.2 18.0 reduce-scatter.4
  117.9 75.6 reduce-scatter.2
  195.8 31.4 all-reduce.7
  230.7 53.4 all-reduce.5
  288.0 69.7 all-reduce.3
where the time goes:
time: 367 us; the launch traced here: 366 us
  waiting for transfers between devices  217 us (59%)
  blocking collectives  87.8 us (24%)
  matrix products  42.5 us (12%)
  between operations  14.3 us (4%)
    all_gather x1, waiting for transfers between devices, per_device(): portion = lax.all_gather(tokens, 'col', axis=0, tiled=True)  85.1 us
    psum x1, waiting for transfers between devices, per_device(): lax.psum(row_term + first_group * norm_term, ('dp', 'col'))  71.9 us
    psum x1, blocking collectives, per_device(): backward_rows = lax.psum(padded, ('row', 'col')).astype(jnp.bfloat16)  69.2 us
    psum x1, waiting for transfers between devices, per_device(): scale_grad, bgrad_data = lax.psum((scale_terms, bgrad_terms), ('dp', 'row'))  57 us
    dot_general x8, matrix products, contract_product(): lax.dot_general(left, right, (((left_dim,), (right_dim,)), ((), ())), pre...  19.1 us
    dot_general x1, matrix products, per_device(): jnp.dot(portion, frozen_weight, preferred_element_type=jnp.float32)  14.4 us
    psum x1, blocking collectives, per_device(): scale_grad, bgrad_data = lax.psum((scale_terms, bgrad_terms), ('dp', 'row'))  12.1 us
  transfers between devices with their start and end apart: 6, of which 4 were waited for; matrix products, arithmetic and copies ran while one was open for 11% of the time, Pallas kernels for 0%

commit v1 on v0

--- a/solution.py
+++ b/solution.py
@@ -66,7 +66,7 @@
     scale_terms = jnp.sum(grad_out * query_projection, axis=0)
     projection_gradient = (grad_out * col_scale[None, :]).astype(jnp.bfloat16)
     bgrad_terms = contract_product(down_activations, projection_gradient, 0, 0)
-    scale_grad, bgrad_data = lax.psum((scale_terms, bgrad_terms), ("dp", "row"))
+    scale_grad, bgrad_data = lax.psum(lax.psum((scale_terms, bgrad_terms), "dp"), "row")
     grad_mag = scale_grad / col_norm
     norm_coefficient = -scale_grad * magnitude / (col_norm * col_norm * col_norm)
     grad_b = bgrad_data + merged_input_factor * norm_coefficient[None, :]

time: 367 us -> 400 us (1.090)
  waiting for transfers between devices: 217 us -> 253 us
    reduce_scatter x1, waiting for transfers between devices: 0.02 us -> 65.2 us  [per_device(): lax.psum_scatter(base_piece, 'row', scatter_dimension=0, tiled=True)]
    psum x2, waiting for transfers between devices: 59.4 us -> 28.9 us  [the longest x1 28.9 us: per_device(): lax.psum(lax.psum((scale_terms, bgrad_terms), 'dp'), 'row')]
    psum x1, blocking collectives: 12.1 us -> 5 us  [per_device(): lax.psum((scale_terms, bgrad_terms), 'dp')]
  transfers between devices with their start and end apart: 6 -> 6, of which waited for: 4 -> 4; matrix products, arithmetic and copies ran while one was open for 11% -> 8% of each run, Pallas kernels for 0% -> 0%
where the time goes in v1:
time: 400 us
  waiting for transfers between devices  253 us (63%)
  blocking collectives  85.2 us (21%)
  matrix products  41.8 us (10%)
  between operations  14.2 us (4%)
    all_gather x1, waiting for transfers between devices, per_device(): portion = lax.all_gather(tokens, 'col', axis=0, tiled=True)  85.1 us
    psum x1, waiting for transfers between devices, per_device(): lax.psum(row_term + first_group * norm_term, ('dp', 'col'))  72.6 us
    psum x1, blocking collectives, per_device(): backward_rows = lax.psum(padded, ('row', 'col')).astype(jnp.bfloat16)  70.1 us
    reduce_scatter x1, waiting for transfers between devices, per_device(): lax.psum_scatter(base_piece, 'row', scatter_dimension=0, tiled=True)  65.2 us
    psum x1, waiting for transfers between devices, per_device(): lax.psum(lax.psum((scale_terms, bgrad_terms), 'dp'), 'row')  28.9 us
    dot_general x8, matrix products, contract_product(): lax.dot_general(left, right, (((left_dim,), (right_dim,)), ((), ())), pre...  19.6 us
    dot_general x1, matrix products, per_device(): jnp.dot(portion, frozen_weight, preferred_element_type=jnp.float32)  14.4 us
    psum x1, blocking collectives, per_device(): lax.psum((norm_terms, merged_factor_terms), 'row')  10.1 us
  transfers between devices with their start and end apart: 6, of which 4 were waited for; matrix products, arithmetic and copies ran while one was open for 8% of the time, Pallas kernels for 0%

profile of v1, /device:TPU:0, one launch (start us, length us, event | category | flops | bytes accessed | tf_op | source)
XLA Modules:
  0.0 399.9 jit_solution(8748427013280661994)
XLA Ops:
  7.2 0.7 all-gather.2.cloned.1.call-update
  7.9 0.0 reduce-scatter.5.cloned.1.call-start
  8.0 85.1 %all-gather.2.cloned.1.call-done = bf16[1024,2048]{1,0:T(8,128)(2,1)} async-done(((bf16[256,2048]{1,0:T(8,128)(2,1)}), bf16[1024,2048]{1,0:T(8,128)(2,1)}) %all-gather.2.cloned.1.call-update) | async-done | bytes 4194320 | tf_op jit(solution)/shard_map/all_gather | solution.py:43
  93.1 4.0 %fusion.14 = f32[1024,16]{0,1:T(8,128)} fusion(bf16[1024,2048]{1,0:T(8,128)(2,1)} %all-gather.2.cloned.1.call-done, bf16[16,2048]{1,0:T(8,128)(2,1)S(1)} %copy-done), kind=kOutput, calls=%fused_computation.33 | convolution fusion | flops 67108864 | bytes 4325376 | tf_op jit(solution)/shard_map/dot_general | solution.py:11
  97.1 0.0 reduce-scatter.3.cloned.1.call-start
  97.1 14.4 %fusion.13 = f32[1024,2048]{1,0:T(8,128)} fusion(bf16[1024,2048]{1,0:T(8,128)(2,1)} %all-gather.2.cloned.1.call-done, bf16[2048,2048]{1,0:T(8,128)(2,1)} %param.8), kind=kOutput, calls=%fused_computation.32 | convolution fusion | flops 8589934592 | bytes 20971520 | tf_op jit(solution)/shard_map/dot_general | solution.py:44
  111.6 0.0 all-reduce.8.cloned.1.call-start
  111.7 0.6 copy-done.6
  112.2 0.2 reduce-window.4
  112.4 0.1 select_reduce_fusion
  112.5 0.1 fusion.16
  112.6 4.7 %fusion.15 = f32[16,2048]{1,0:T(8,128)S(1)} fusion(bf16[16,2048]{1,0:T(8,128)(2,1)S(1)} %copy-done, bf16[2048,2048]{1,0:T(8,128)(2,1)} %param.8), kind=kOutput, calls=%fused_computation.34 | convolution fusion | flops 134217728 | bytes 8585216 | tf_op jit(solution)/shard_map/dot_general | solution.py:38
  117.3 0.8 convolution_add_fusion.1
  118.1 5.9 %multiply_reduce_fusion = f32[2048]{0:T(1024)S(1)} fusion(bf16[2048,2048]{1,0:T(8,128)(2,1)} %param.8, bf16[16,2048]{1,0:T(8,128)(2,1)S(1)} %copy-done, bf16[16,2048]{1,0:T(8,128)(2,1)S(1)} %copy-done.2), kind=kOutput, calls=%fused_computation | convolution fusion | flops 150992896 | bytes 8527872 | tf_op jit(solution)/shard_map/dot_general | solution.py:11
  124.1 65.2 %reduce-scatter.3.cloned.1.call-done = f32[256,2048]{1,0:T(8,128)} async-done(((f32[1024,2048]{1,0:T(8,128)}), f32[256,2048]{1,0:T(8,128)}) %reduce-scatter.3.cloned.1.call-update) | async-done | bytes 2097168 | tf_op jit(solution)/shard_map/reduce_scatter | solution.py:47
  189.3 2.1 multiply_reduce_fusion.1
  191.4 5.0 %psum.57 = f32[2048]{0:T(1024)S(1)} all-reduce(f32[2048]{0:T(1024)S(1)} %get-tuple-element.11), channel_id=1, replica_groups=mesh['dp'=2,'row'=4,'col'=4] {'dp'}, use_global_device_ids=true, to_apply=%region_7.8 | all-reduce | flops 2048 | bytes 16384 | tf_op jit(solution)/shard_map/psum | solution.py:69
  196.4 10.1 %all-reduce = (f32[2048]{0:T(1024)S(1)}, f32[2048]{0:T(1024)S(1)}) all-reduce(f32[2048]{0:T(1024)S(1)} %multiply_reduce_fusion, f32[2048]{0:T(1024)S(1)} %psum.57), channel_id=1, replica_groups=mesh['dp'=2,'row'=4,'col'=4] {'row'}, use_global_device_ids=true, to_apply=%region_3.0 | all-reduce | flops 4096 | bytes 32768 | tf_op jit(solution)/shard_map/psum | solution.py:50
  206.6 0.6 fusion.6
  207.2 5.7 %fusion.3 = f32[16,2048]{1,0:T(8,128)S(1)} fusion(bf16[2048,2048]{1,0:T(8,128)(2,1)} %param.8, bf16[16,2048]{1,0:T(8,128)(2,1)S(1)} %copy-done.2, f32[2048]{0:T(1024)S(1)} %get-tuple-element.8), kind=kOutput, calls=%fused_computation.16 | convolution fusion | flops 134316032 | bytes 8593408 | tf_op jit(solution)/shard_map/dot_general | solution.py:11
  212.9 0.1 fusion.2
  213.0 1.1 fusion.1
  214.1 0.0 all-reduce.10.cloned.1.call-start
  214.2 1.2 multiply_convert_fusion.1
  215.4 1.7 convolution_dynamic-update-slice_fusion
  217.1 0.2 fusion
  217.3 70.1 %psum.59 = bf16[1024,16]{1,0:T(8,128)(2,1)S(1)} all-reduce(f32[1024,16]{1,0:T(8,128)S(1)} %convolution_dynamic-update-slice_fusion), channel_id=1, replica_groups=mesh['dp'=2,'row'=4,'col'=4] {'row','col'}, use_global_device_ids=true, to_apply=%region_9.10 | all-reduce | flops 16384 | bytes 98304 | tf_op jit(solution)/shard_map/psum | solution.py:80
  287.5 0.9 convolution_add_fusion.3
  288.4 28.9 %all-reduce.10.cloned.1.call-done = (f32[16,2048]{1,0:T(8,128)}, f32[16,2048]{1,0:T(8,128)}) async-done(((f32[16,2048]{1,0:T(8,128)}, f32[16,2048]{1,0:T(8,128)}), (f32[16,2048]{1,0:T(8,128)}, f32[16,2048]{1,0:T(8,128)})) %all-reduce.10.cloned.1.call-update) | async-done | bytes 262160 | tf_op jit(solution)/shard_map/psum | solution.py:69
  317.3 1.6 multiply_add_fusion
  318.9 72.6 %all-reduce.6.cloned.1.call-done = f32[16,2048]{1,0:T(8,128)} async-done(((f32[16,2048]{1,0:T(8,128)}), f32[16,2048]{1,0:T(8,128)}) %all-reduce.6.cloned.1.call-update) | async-done | bytes 131088 | tf_op jit(solution)/shard_map/psum | solution.py:92
  391.5 1.6 copy.16
  (26 shorter events, 0.3 us)
Async XLA Ops:
  7.2 85.9 %copy-start = (bf16[16,2048]{1,0:T(8,128)(2,1)S(1)}, bf16[16,2048]{1,0:T(8,128)(2,1)}, u32[]{:S(2)}) copy-start(bf16[16,2048]{1,0:T(8,128)(2,1)} %param.9) | copy-start | bytes 196612
  7.2 85.9 %all-gather.2.cloned.1.call-start = ((), (), s32[]{:S(2)}) async-start(), calls=%async_computation.2 | async-start | bytes 5242880 | tf_op jit(solution)/shard_map/all_gather | solution.py:43
  7.9 116.1 %reduce-scatter.5.cloned.1.call-start = ((), (), s32[]{:S(2)}) async-start(), calls=%async_computation.4 | async-start | bytes 81920 | tf_op jit(solution)/shard_map/reduce_scatter | solution.py:48
  97.1 92.2 %reduce-scatter.3.cloned.1.call-start = ((), (), s32[]{:S(2)}) async-start(), calls=%async_computation.3 | async-start | bytes 10485760 | tf_op jit(solution)/shard_map/reduce_scatter | solution.py:47
  111.6 0.7 copy-start.6
  111.6 175.8 %all-reduce.8.cloned.1.call-start = ((), (), s32[]{:S(2)}) async-start(), calls=%async_computation.6 | async-start | bytes 262144 | tf_op jit(solution)/shard_map/psum | solution.py:69
  112.6 4.7 %copy-start.2 = (bf16[16,2048]{1,0:T(8,128)(2,1)S(1)}, bf16[16,2048]{1,0:T(8,128)(2,1)}, u32[]{:S(2)}) copy-start(bf16[16,2048]{1,0:T(8,128)(2,1)} %param.10) | copy-start | bytes 196612
  118.1 71.2 %copy-start.3 = (bf16[256,2048]{1,0:T(8,128)(2,1)S(1)}, bf16[256,2048]{1,0:T(8,128)(2,1)}, u32[]{:S(2)}) copy-start(bf16[256,2048]{1,0:T(8,128)(2,1)} %param.12) | copy-start | bytes 3145732
  124.0 82.6 %copy-start.5 = (f32[2048]{0:T(1024)S(1)}, f32[2048]{0:T(1024)}, u32[]{:S(2)}) copy-start(f32[2048]{0:T(1024)} %param.11) | copy-start | bytes 24580
  207.2 5.8 %copy-start.4 = (f32[256,16]{0,1:T(8,128)S(1)}, f32[256,16]{0,1:T(8,128)}, u32[]{:S(2)}) copy-start(f32[256,16]{0,1:T(8,128)} %reduce-scatter.5.cloned.1.call-done) | copy-start | bytes 49156
  214.1 73.4 %copy-start.1 = (bf16[256,2048]{1,0:T(8,128)(2,1)S(1)}, bf16[256,2048]{1,0:T(8,128)(2,1)}, u32[]{:S(2)}) copy-start(bf16[256,2048]{1,0:T(8,128)(2,1)} %param.7) | copy-start | bytes 3145732
  214.1 103.2 %all-reduce.10.cloned.1.call-start = ((), (), s32[]{:S(2)}) async-start(), calls=%async_computation.7 | async-start | bytes 524288 | tf_op jit(solution)/shard_map/psum | solution.py:69
  287.4 104.1 %all-reduce.6.cloned.1.call-start = ((), (), s32[]{:S(2)}) async-start(), calls=%async_computation.5 | async-start | bytes 262144 | tf_op jit(solution)/shard_map/psum | solution.py:92
Sparse Core Ops, SparseCore 0:
  9.6 83.4 all-gather.1
  97.2 18.0 reduce-scatter.4
  117.9 71.3 reduce-scatter.2
  214.3 21.6 all-reduce.7
  287.5 29.7 all-reduce.9
  321.1 70.4 all-reduce.5
